TPU v7x, 32 devices: a whole 2x2x4 slice. The times are simulated.
32 devices in a mesh: ends: 2 (over x), dp: 4 (over y, core), tp: 4 (over z).
Axes of the slice: x: 2, y: 2, z: 4, core: 2. Of those that a mesh axis runs over, the one named last changes fastest.
Arguments:
- grad: bfloat16 [2, 4, 4096, 3072], P('ends', 'dp', 'tp'), may hold values from -1800 to 1800
- master: float32 [4, 1024, 3072], P('tp', ('ends', 'dp')), may hold values from -3 to 3
- moment: float32 [4, 1024, 3072], P('tp', ('ends', 'dp')), may hold values from -3 to 3
- second: float32 [4, 1024, 3072], P('tp', ('ends', 'dp')), may hold values from 0.01 to 1
Outputs:
- weights: bfloat16 [4096, 3072], P('tp')
- master_out: float32 [4, 1024, 3072], P('tp', ('ends', 'dp'))
- moment_out: float32 [4, 1024, 3072], P('tp', ('ends', 'dp'))
- second_out: float32 [4, 1024, 3072], P('tp', ('ends', 'dp'))
All inputs are finite; a program needn't handle non-finite values.
Results may differ from a plain program's by a relative error of at most 0.0034.
Values may be sent and summed in bfloat16 or wider, within the bound.
A program may use at most 128 MiB of HBM per device.

v0:
```python
import jax
import jax.numpy as jnp
from jax import lax
from jax.sharding import PartitionSpec as P

STEP = 10


def per_device(grad, master, moment, second):
    rows_tp = grad.shape[2]
    width = grad.shape[3]
    local = grad[0, 0].astype(jnp.float32)
    summed = lax.psum_scatter(
        local.astype(jnp.bfloat16), ("ends", "dp"), scatter_dimension=0, tiled=True
    ).astype(jnp.float32)
    squares = lax.psum(jnp.sum(summed * summed), ("ends", "dp", "tp"))
    vocab_total = rows_tp * lax.axis_size("tp")
    factor = jnp.minimum(
        jnp.float32(1.0), jnp.sqrt(jnp.float32(vocab_total * width)) / (jnp.sqrt(squares) + 1e-06)
    )
    clipped = factor * summed
    moment_out = 0.9 * moment[0] + 0.1 * clipped
    second_out = 0.999 * second[0] + 0.001 * clipped * clipped
    update = moment_out / (1.0 - 0.9**STEP) / (jnp.sqrt(second_out / (1.0 - 0.999**STEP)) + 1e-08)
    master_out = master[0] - 0.01 * (update + 0.1 * master[0])
    rounded = master_out.astype(jnp.bfloat16)
    weights = lax.all_gather(rounded, ("ends", "dp"), axis=0, tiled=True)
    return (weights, master_out[None], moment_out[None], second_out[None])


def solution(mesh):
    return jax.shard_map(
        per_device,
        mesh=mesh,
        in_specs=(
            P("ends", "dp", "tp", None),
            P("tp", ("ends", "dp"), None),
            P("tp", ("ends", "dp"), None),
            P("tp", ("ends", "dp"), None),
        ),
        out_specs=(
            P("tp", None),
            P("tp", ("ends", "dp"), None),
            P("tp", ("ends", "dp"), None),
            P("tp", ("ends", "dp"), None),
        ),
        check_vma=False,
    )
```

profile of v0, /device:TPU:0, one launch (start us, length us, event | category | flops | bytes accessed | tf_op | source)
XLA Modules:
  0.0 182.9 jit_solution(17955837201795588932)
XLA Ops:
  7.2 0.0 reduce-scatter.2.cloned.1.call-start
  7.2 0.0 copy-start
  7.2 0.0 copy-start.1
  7.2 0.7 reduce-scatter.2.cloned.1.call-update
  7.9 0.0 all-gather.2.cloned.1.call-start
  7.9 67.9 %reduce-scatter.2.cloned.1.call-done = bf16[128,3072]{1,0:T(8,128)(2,1)} async-done(((bf16[1024,3072]{1,0:T(8,128)(2,1)}), bf16[128,3072]{1,0:T(8,128)(2,1)}) %reduce-scatter.2.cloned.1.call-update) | async-done | bytes 786448 | tf_op jit(solution)/shard_map/reduce_scatter | solution.py:13
  75.8 2.1 %fusion.2 = f32[]{:T(128)} fusion(bf16[128,3072]{1,0:T(8,128)(2,1)} %reduce-scatter.2.cloned.1.call-done), kind=kLoop, calls=%fused_computation.5 | loop fusion | flops 1179647 | bytes 786436 | tf_op jit(solution)/shard_map/reduce_sum | solution.py:16
  78.0 39.5 %psum.7 = f32[]{:T(128)} all-reduce(f32[]{:T(128)} %fusion.2), channel_id=1, replica_groups=mesh['ends'=2,'dp'=4,'tp'=4] {'ends','dp','tp'}, use_global_device_ids=true, to_apply=%region_2.0 | all-reduce | flops 1 | bytes 8 | tf_op jit(solution)/shard_map/psum | solution.py:16
  118.2 0.0 copy-done
  118.2 0.0 copy-done.1
  118.2 5.4 %fusion.8 = (bf16[128,3072]{1,0:T(8,128)(2,1)}, f32[128,3072]{1,0:T(8,128)}, f32[1,128,3072]{2,1,0:T(8,128)}, f32[1,128,3072]{2,1,0:T(8,128)}) fusion(f32[1,128,3072]{2,1,0:T(8,128)S(1)} %copy-done, bf16[128,3072]{1,0:T(8,128)(2,1)} %reduce-scatter.2.cloned.1.call-done, f32[]{:T(128)S(6)} %min_shard_map.3, f32[1,128,3072]{2,1,0:T(8,128)S(1)} %copy-done.1, ...), kind=kLoop, calls=%fused_computation.13 | loop fusion | flops 7077888 | bytes 11010052 | tf_op jit(solution)/shard_map/convert_element_type | solution.py:26
  123.6 0.0 all-gather.2.cloned.1.call-update
  123.6 46.5 %all-gather.2.cloned.1.call-done = bf16[1024,3072]{1,0:T(8,128)(2,1)} async-done(((bf16[128,3072]{1,0:T(8,128)(2,1)}), bf16[1024,3072]{1,0:T(8,128)(2,1)}) %all-gather.2.cloned.1.call-update) | async-done | bytes 6291472 | tf_op jit(solution)/shard_map/all_gather | solution.py:27
  170.1 5.9 %copy.9 = bf16[1024,3072]{1,0:T(8,128)(2,1)} copy(bf16[1024,3072]{1,0:T(8,128)(2,1)} %all-gather.2.cloned.1.call-done) | data formatting | bytes 12582912
Async XLA Ops:
  7.2 68.7 %reduce-scatter.2.cloned.1.call-start = ((), (), s32[]{:S(2)}) async-start(), calls=%async_computation.1 | async-start | bytes 7077888 | tf_op jit(solution)/shard_map/reduce_scatter | solution.py:13
  7.2 111.0 %copy-start = (f32[1,128,3072]{2,1,0:T(8,128)S(1)}, f32[1,128,3072]{2,1,0:T(8,128)}, u32[]{:S(2)}) copy-start(f32[1,128,3072]{2,1,0:T(8,128)} %param.7) | copy-start | bytes 4718596
  7.2 111.0 %copy-start.1 = (f32[1,128,3072]{2,1,0:T(8,128)S(1)}, f32[1,128,3072]{2,1,0:T(8,128)}, u32[]{:S(2)}) copy-start(f32[1,128,3072]{2,1,0:T(8,128)} %param.6) | copy-start | bytes 4718596
  7.9 162.2 %all-gather.2.cloned.1.call-start = ((), (), s32[]{:S(2)}) async-start(), calls=%async_computation.2 | async-start | bytes 7077888 | tf_op jit(solution)/shard_map/all_gather | solution.py:27
Sparse Core Ops, SparseCore 0:
  11.4 64.4 reduce-scatter.1
  123.7 46.2 all-gather.1
where the time goes:
time: 183 us
  waiting for transfers between devices  115 us (63%)
  blocking collectives  39.5 us (22%)
  between operations  14.8 us (8%)
  other arithmetic  7.52 us (4%)
  local copies, waits for them, and re-layouts  5.94 us (3%)
    reduce_scatter x1, waiting for transfers between devices, per_device(): lax.psum_scatter(local.astype(jnp.bfloat16), ('ends', 'dp'), scatter_dime...  67.9 us
    all_gather x1, waiting for transfers between devices, per_device(): weights = lax.all_gather(rounded, ('ends', 'dp'), axis=0, tiled=True)  46.5 us
    psum x1, blocking collectives, per_device(): squares = lax.psum(jnp.sum(summed * summed), ('ends', 'dp', 'tp'))  39.5 us
    unnamed x5, local copies, waits for them, and re-layouts  5.94 us
    convert_element_type x1, other arithmetic, per_device(): rounded = master_out.astype(jnp.bfloat16)  5.38 us
  transfers between devices with their start and end apart: 2, of which 2 were waited for; matrix products, arithmetic and copies ran while one was open for 0% of the time, Pallas kernels for 0%

commit v1 on v0

v1 whole, which is shorter than its diff:
```python
import functools
import math

import jax
import jax.numpy as jnp
from jax import lax
from jax.experimental import pallas as pl
from jax.experimental.pallas import tpu as pltpu
from jax.sharding import PartitionSpec as P

STEP = 10
MESH = pl.DeviceIdType.MESH
F32 = jnp.float32
BF16 = jnp.bfloat16


def remote(src, dst, send, recv, device):
    return pltpu.make_async_remote_copy(
        src_ref=src, dst_ref=dst, send_sem=send, recv_sem=recv, device_id=device, device_id_type=MESH
    )


def kernel(cfg, grad, master, moment, second, w_out, master_out, moment_out, second_out, *scratch):
    ends, ys, tps, rows, width, pieces, staged = cfg
    if staged:
        w_hbm, (w_out, w_sem), scratch = w_out, scratch[-2:], scratch[:-2]
    (own, peer, part1, land1, part2, land2, total, st0, st1, st2, squares,
     own_sem, st_sem, peer_s, peer_r, s1, r1, s2, r2, ns, nr, a_s, a_r, b_s, b_r, f_s, f_r, p_s, p_r) = scratch
    e, dp, t = lax.axis_index("ends"), lax.axis_index("dp"), lax.axis_index("tp")
    y, c = dp // 2, lax.rem(dp, 2)
    ch = rows // pieces
    devices = ends * ys * 2 * tps
    square = ends == ys
    n1, n2 = (ends, ys) if square else (ys, ends)

    def place(core, da, db):
        if square:
            ends_first = core == 0
            de, dy = jnp.where(ends_first, da, db), jnp.where(ends_first, db, da)
        else:
            de, dy = db, da
        return lax.rem(e + de, ends), lax.rem(y + dy, ys)

    def first_row(core, da, db):
        ee, yy = place(core, da, db)
        return pl.multiple_of(((ee * ys + yy) * 2 + core) * rows, rows)

    def at(da, db):
        ee, yy = place(c, da, db)
        return {"ends": ee, "dp": yy * 2 + c}

    partner = {"dp": y * 2 + (1 - c)}
    shifts1, shifts2 = range(1, n1), range(1, n2)
    order = (
        [(da, db) for da in shifts1 for db in shifts2]
        + [(0, db) for db in shifts2]
        + [(da, 0) for da in shifts1]
        + [(0, 0)]
    )
    slot = lambda da, db: da * n2 + db
    part = lambda k: pl.ds(k * ch, ch)

    def own_copy(da, db, k):
        i = slot(da, db)
        r = pl.multiple_of(first_row(c, da, db) + k * ch, ch)
        return pltpu.make_async_copy(grad.at[pl.ds(r, ch)], own.at[i, part(k)], own_sem.at[i * pieces + k])

    for da, db in order:
        for k in range(pieces):
            own_copy(da, db, k).start()
    state_copies = [
        pltpu.make_async_copy(src, dst, st_sem.at[i])
        for i, (src, dst) in enumerate(((master, st0), (moment, st1), (second, st2)))
    ]

    me = (e * (ys * 2) + dp) * tps + t

    def device_of(i):
        return {"ends": i // (ys * 2 * tps), "dp": lax.rem(i // tps, ys * 2), "tp": lax.rem(i, tps)}

    barrier = pltpu.get_barrier_semaphore()

    @pl.loop(1, devices)
    def _(d):
        pl.semaphore_signal(barrier, inc=1, device_id=device_of(lax.rem(me + d, devices)), device_id_type=MESH)

    pl.semaphore_wait(barrier, devices - 1)

    for da, db in order:
        for k in range(pieces):
            i = slot(da, db)
            r = pl.multiple_of(first_row(1 - c, da, db) + k * ch, ch)
            remote(grad.at[pl.ds(r, ch)], peer.at[i, part(k)], peer_s, peer_r.at[i * pieces + k], partner).start()
    for copy in state_copies:
        copy.start()

    def chip_sum(da, db, k):
        i = slot(da, db)
        own_copy(da, db, k).wait()
        remote(peer.at[i, part(k)], peer.at[i, part(k)], peer_s, peer_r.at[i * pieces + k], partner).wait_recv()
        return own[i, part(k), :].astype(F32) + peer[i, part(k), :].astype(F32)

    def copy1(da, db, k):
        i = (da - 1) * n2 + db
        return remote(part1.at[i, part(k)], land1.at[i, part(k)], s1, r1.at[i * pieces + k], at(da, 0))

    def copy2(db, k):
        i = db - 1
        return remote(part2.at[i, part(k)], land2.at[i, part(k)], s2, r2.at[i * pieces + k], at(0, db))

    def send1(da, db, k):
        part1[(da - 1) * n2 + db, part(k), :] = chip_sum(da, db, k).astype(BF16)
        copy1(da, db, k).start()

    def sum1(db, k):
        value = chip_sum(0, db, k)
        for da in shifts1:
            copy1(da, db, k).wait_recv()
            value = value + land1[(da - 1) * n2 + db, part(k), :].astype(F32)
        return value

    for k in range(pieces):
        for da in shifts1:
            for db in shifts2:
                send1(da, db, k)
    for k in range(pieces):
        for da in shifts1:
            send1(da, 0, k)
        for db in shifts2:
            part2[db - 1, part(k), :] = sum1(db, k).astype(BF16)
            copy2(db, k).start()
    acc = jnp.zeros((8, width), F32)
    for k in range(pieces):
        value = sum1(0, k)
        for db in shifts2:
            copy2(db, k).wait_recv()
            value = value + land2[db - 1, part(k), :].astype(F32)
        total[part(k), :] = value
        value = value * value
        for r in range(0, ch, 8):
            acc = acc + value[r : r + 8, :]

    mine = acc[:, :128]
    for j in range(128, width, 128):
        mine = mine + acc[:, j : j + 128]
    squares[me] = mine

    @pl.loop(1, devices)
    def _(d):
        remote(squares.at[me], squares.at[me], ns, nr, device_of(lax.rem(me + d, devices))).start()

    others = squares.at[pl.ds(0, devices - 1)]
    everyone = remote(others, others, ns, nr, partner)
    for copy in state_copies:
        copy.wait()
    everyone.wait_recv()
    everyone.wait_send()
    norm2 = jnp.full((8, 128), jnp.sum(jnp.sum(squares[...], axis=0)), F32)
    entries = float(tps * ends * ys * 2 * rows * width)
    factor = jnp.minimum(F32(1.0), F32(math.sqrt(entries)) / (jnp.sqrt(norm2) + 1e-06))[:1, :1]

    my_row = first_row(c, 0, 0)

    def piece_of(da, db, k):
        return w_out.at[pl.ds(pl.multiple_of(first_row(c, da, db) + k * ch, ch), ch)]

    def copy_a(da, src, k):
        return remote(src, src, a_s, a_r.at[(da - 1) * pieces + k], at(da, 0))

    def copy_b(db, src, k):
        return remote(src, src, b_s, b_r.at[(db - 1) * pieces + k], at(0, db))

    def copy_f(da, db, src, k):
        return remote(src, src, f_s, f_r.at[((da - 1) * (n2 - 1) + db - 1) * pieces + k], at(0, db))

    def copy_p(src):
        return remote(src, src, p_s, p_r, partner)

    for k in range(pieces):
        @pl.loop(0, ch // 16)
        def _(g):
            at_row = pl.multiple_of(k * ch + g * 16, 16)
            here = pl.ds(at_row, 16)
            clipped = factor * total[here, :]
            m = 0.9 * st1[here, :] + 0.1 * clipped
            v = 0.999 * st2[here, :] + 0.001 * clipped * clipped
            update = m / (1.0 - 0.9**STEP) / (jnp.sqrt(v / (1.0 - 0.999**STEP)) + 1e-08)
            w = st0[here, :]
            w = w - 0.01 * (update + 0.1 * w)
            moment_out[here, :] = m
            second_out[here, :] = v
            master_out[here, :] = w
            w_out[pl.ds(pl.multiple_of(my_row + at_row, 16), 16), :] = w.astype(BF16)

        src = piece_of(0, 0, k)
        for da in shifts1:
            copy_a(da, src, k).start()
        for db in shifts2:
            copy_b(db, src, k).start()
        copy_p(src).start()

    for k in range(pieces):
        for da in shifts1:
            src = piece_of(n1 - da, 0, k)
            copy_a(da, src, k).wait_recv()
            for db in shifts2:
                copy_f(da, db, src, k).start()
            copy_p(src).start()
        for db in shifts2:
            src = piece_of(0, n2 - db, k)
            copy_b(db, src, k).wait_recv()
            copy_p(src).start()
    for k in range(pieces):
        for da in shifts1:
            for db in shifts2:
                src = piece_of(n1 - da, n2 - db, k)
                copy_f(da, db, src, k).wait_recv()
                copy_p(src).start()

    half = w_out.at[pl.ds(0, n1 * n2 * rows)]
    remote(half, half, p_s, p_r, partner).wait_recv()
    remote(half, half, p_s, p_r, partner).wait_send()
    remote(peer, peer, peer_s, peer_r.at[0], partner).wait_send()
    remote(part1, land1, s1, r1.at[0], partner).wait_send()
    remote(part2, land2, s2, r2.at[0], partner).wait_send()
    for sem, count, recv in ((a_s, n1 - 1, a_r), (b_s, n2 - 1, b_r), (f_s, (n1 - 1) * (n2 - 1), f_r)):
        ref = w_out.at[pl.ds(0, count * rows)]
        remote(ref, ref, sem, recv.at[0], partner).wait_send()
    if staged:
        final = pltpu.make_async_copy(w_out, w_hbm, w_sem)
        final.start()
        final.wait()


def per_device(mesh, grad, master, moment, second):
    ends, dps, tps = (mesh.shape[name] for name in ("ends", "dp", "tp"))
    ys = dps // 2
    rows_tp, width = grad.shape[2:]
    rows = rows_tp // (ends * dps)
    pieces = 4 if rows % 64 == 0 else 1
    n1, n2 = (ends, ys) if ends == ys else (ys, ends)
    blocks = n1 * n2
    devices = ends * dps * tps
    dma = lambda n: pltpu.SemaphoreType.DMA((n,))
    one = pltpu.SemaphoreType.DMA
    block = lambda n, dtype=BF16: pltpu.VMEM((n, rows, width), dtype)
    state = lambda: pltpu.VMEM((rows, width), F32)
    scratch = [
        block(blocks), block(blocks),
        block((n1 - 1) * n2), block((n1 - 1) * n2),
        block(n2 - 1), block(n2 - 1),
        state(), state(), state(), state(),
        pltpu.VMEM((devices, 8, 128), F32),
        dma(blocks * pieces), dma(3), one, dma(blocks * pieces),
        one, dma((n1 - 1) * n2 * pieces), one, dma((n2 - 1) * pieces),
        one, one,
        one, dma((n1 - 1) * pieces), one, dma((n2 - 1) * pieces),
        one, dma((n1 - 1) * (n2 - 1) * pieces),
        one, one,
    ]
    block_bytes = rows * width * 2
    staged = rows_tp * width * 2 > 8 << 20
    if staged:
        scratch += [pltpu.VMEM((rows_tp, width), BF16), one]
    limit = block_bytes * (2 * blocks + 2 * (n1 - 1) * n2 + 2 * (n2 - 1) + 8 + staged * ends * dps) + devices * 4096 + (3 << 20)
    stays = pl.BlockSpec(memory_space=pltpu.HBM)
    vmem = pl.BlockSpec(memory_space=pltpu.VMEM)
    weights, master_out, moment_out, second_out = pl.pallas_call(
        functools.partial(kernel, (ends, ys, tps, rows, width, pieces, staged)),
        out_shape=(
            (pltpu.HBM if staged else pltpu.VMEM)((rows_tp, width), BF16),
            pltpu.VMEM((rows, width), F32),
            pltpu.VMEM((rows, width), F32),
            pltpu.VMEM((rows, width), F32),
        ),
        in_specs=[stays] * 4,
        out_specs=(stays if staged else vmem,) + (vmem,) * 3,
        scratch_shapes=scratch,
        compiler_params=pltpu.CompilerParams(collective_id=0, has_side_effects=True, vmem_limit_bytes=limit),
        name="sum_update_gather",
    )(*(pltpu.with_memory_space_constraint(x, pltpu.HBM) for x in (grad[0, 0], master[0], moment[0], second[0])))
    return (weights, master_out[None], moment_out[None], second_out[None])


def solution(mesh):
    rows = P("tp", ("ends", "dp"), None)
    return jax.shard_map(
        functools.partial(per_device, mesh),
        mesh=mesh,
        in_specs=(P("ends", "dp", "tp", None), rows, rows, rows),
        out_specs=(P("tp", None), rows, rows, rows),
        check_vma=False,
    )
```

time: 183 us -> 77.3 us (0.42)
  waiting for transfers between devices: 115 us -> 0 us
  Pallas kernels: 0 us -> 70.4 us
  blocking collectives: 39.5 us -> 0 us
  between operations: 14.8 us -> 0.64 us
  other arithmetic: 7.52 us -> 0 us
    pallas_call x0 -> x1, Pallas kernels: none -> 70.4 us  [per_device(): pl.pallas_call(functools.partial(kernel, (ends, ys, tps, rows, width, pie...]
    reduce_scatter x1 -> x0, waiting for transfers between devices: 67.9 us -> none  [per_device(): lax.psum_scatter(local.astype(jnp.bfloat16), ('ends', 'dp'), scatter_dime...]
    all_gather x1 -> x0, waiting for transfers between devices: 46.5 us -> none  [per_device(): weights = lax.all_gather(rounded, ('ends', 'dp'), axis=0, tiled=True)]
    psum x1 -> x0, blocking collectives: 39.5 us -> none  [per_device(): squares = lax.psum(jnp.sum(summed * summed), ('ends', 'dp', 'tp'))]
    convert_element_type x1 -> x0, other arithmetic: 5.38 us -> none  [per_device(): rounded = master_out.astype(jnp.bfloat16)]
    reduce_sum x1 -> x0, other arithmetic: 2.14 us -> none  [per_device(): squares = lax.psum(jnp.sum(summed * summed), ('ends', 'dp', 'tp'))]
    unnamed x5 -> x4, local copies, waits for them, and re-layouts: 5.94 us -> 6.13 us
  transfers between devices with their start and end apart: 2 -> 0, of which waited for: 2 -> 0; matrix products, arithmetic and copies ran while one was open for 0% -> 0% of each run, Pallas kernels for 0% -> 0%
where the time goes in v1:
time: 77.3 us; the launch traced here: 77.2 us
  Pallas kernels  70.4 us (91%)
  local copies, waits for them, and re-layouts  6.13 us (8%)
    pallas_call x1, Pallas kernels, per_device(): pl.pallas_call(functools.partial(kernel, (ends, ys, tps, rows, width, pie...  70.4 us
    unnamed x4, local copies, waits for them, and re-layouts  6.13 us

profile of v1, /device:TPU:0, one launch (start us, length us, event | category | flops | bytes accessed | tf_op | source)
XLA Modules:
  0.0 77.2 jit_solution(776581037232654)
XLA Ops:
  0.6 70.4 %sum_update_gather.1 = (bf16[1024,3072]{1,0:T(8,128)(2,1)S(1)}, f32[128,3072]{1,0:T(8,128)S(1)}, f32[128,3072]{1,0:T(8,128)S(1)}, f32[128,3072]{1,0:T(8,128)S(1)}) custom-call(bf16[1024,3072]{1,0:T(8,128)(2,1)} %bitcast.10, f32[128,3072]{1,0:T(8,128)} %bitcast.11, f32[128,3072]{1,0:T(8,128)} %bitcast.12, f32[128,3072]{1,0:T(8,128)} %bitcast.13), custom_call_target="tpu_custom_call" | custom-call | tf_op jit(solution)/shard_map/sum_update_gather/pallas_call | solution.py:268
  71.0 2.7 %copy.12 = bf16[1024,3072]{1,0:T(8,128)(2,1)} copy(bf16[1024,3072]{1,0:T(8,128)(2,1)S(1)} %get-tuple-element.12) | data formatting | bytes 12582912
  73.8 1.1 %copy.13 = f32[1,128,3072]{2,1,0:T(8,128)} copy(f32[1,128,3072]{2,1,0:T(8,128)S(1)} %bitcast.9) | data formatting | bytes 3145728
  74.9 1.1 %copy.14 = f32[1,128,3072]{2,1,0:T(8,128)} copy(f32[1,128,3072]{2,1,0:T(8,128)S(1)} %bitcast.8) | data formatting | bytes 3145728
  76.0 1.1 %copy.15 = f32[1,128,3072]{2,1,0:T(8,128)} copy(f32[1,128,3072]{2,1,0:T(8,128)S(1)} %bitcast.7) | data formatting | bytes 3145728

commit v2 on v1

--- a/solution.py
+++ b/solution.py
@@ -143,7 +143,7 @@
     mine = acc[:, :128]
     for j in range(128, width, 128):
         mine = mine + acc[:, j : j + 128]
-    squares[me] = mine
+    squares[me] = jnp.sum(mine, axis=0, keepdims=True)
 
     @pl.loop(1, devices)
     def _(d):
@@ -230,6 +230,19 @@
         final = pltpu.make_async_copy(w_out, w_hbm, w_sem)
         final.start()
         final.wait()
+
+
+def put_out(*refs):
+    count = len(refs) // 2
+    sems = refs[-1]
+    copies = [
+        pltpu.make_async_copy(src, dst, sems.at[i])
+        for i, (src, dst) in enumerate(zip(refs[:count], refs[count : 2 * count]))
+    ]
+    for copy in copies:
+        copy.start()
+    for copy in copies:
+        copy.wait()
 
 
 def per_device(mesh, grad, master, moment, second):
@@ -250,7 +263,7 @@
         block((n1 - 1) * n2), block((n1 - 1) * n2),
         block(n2 - 1), block(n2 - 1),
         state(), state(), state(), state(),
-        pltpu.VMEM((devices, 8, 128), F32),
+        pltpu.VMEM((devices, 1, 128), F32),
         dma(blocks * pieces), dma(3), one, dma(blocks * pieces),
         one, dma((n1 - 1) * n2 * pieces), one, dma((n2 - 1) * pieces),
         one, one,
@@ -265,7 +278,8 @@
     limit = block_bytes * (2 * blocks + 2 * (n1 - 1) * n2 + 2 * (n2 - 1) + 8 + staged * ends * dps) + devices * 4096 + (3 << 20)
     stays = pl.BlockSpec(memory_space=pltpu.HBM)
     vmem = pl.BlockSpec(memory_space=pltpu.VMEM)
-    weights, master_out, moment_out, second_out = pl.pallas_call(
+    vmem_any = pl.BlockSpec(memory_space=pl.ANY)
+    results = pl.pallas_call(
         functools.partial(kernel, (ends, ys, tps, rows, width, pieces, staged)),
         out_shape=(
             (pltpu.HBM if staged else pltpu.VMEM)((rows_tp, width), BF16),
@@ -279,6 +293,18 @@
         compiler_params=pltpu.CompilerParams(collective_id=0, has_side_effects=True, vmem_limit_bytes=limit),
         name="sum_update_gather",
     )(*(pltpu.with_memory_space_constraint(x, pltpu.HBM) for x in (grad[0, 0], master[0], moment[0], second[0])))
+    first = 1 if staged else 0
+    here = results[first:]
+    out = pl.pallas_call(
+        put_out,
+        out_shape=tuple(pltpu.HBM(x.shape, x.dtype) for x in here),
+        in_specs=[vmem_any] * len(here),
+        out_specs=(stays,) * len(here),
+        scratch_shapes=[dma(len(here))],
+        compiler_params=pltpu.CompilerParams(vmem_limit_bytes=1 << 20),
+        name="put_out",
+    )(*(pltpu.with_memory_space_constraint(x, pltpu.VMEM) for x in here))
+    weights, master_out, moment_out, second_out = tuple(results[:first]) + tuple(out)
     return (weights, master_out[None], moment_out[None], second_out[None])
 
 

time: 77.3 us -> 74.6 us (0.965)
  local copies, waits for them, and re-layouts: 6.13 us -> 0 us
  Pallas kernels: 70.4 us -> 73.8 us
    unnamed x4 -> x0, local copies, waits for them, and re-layouts: 6.13 us -> none
    pallas_call x0 -> x1, Pallas kernels: none -> 4.2 us  [per_device(): pl.pallas_call(put_out, out_shape=tuple((pltpu.HBM(x.shape, x.dtype) for...]
    pallas_call x1, Pallas kernels: 70.4 us -> 69.6 us  [per_device(): pl.pallas_call(functools.partial(kernel, (ends, ys, tps, rows, width, pie...]
where the time goes in v2:
time: 74.6 us; the launch traced here: 74.4 us
  Pallas kernels  73.8 us (99%)
    pallas_call x1, Pallas kernels, per_device(): pl.pallas_call(functools.partial(kernel, (ends, ys, tps, rows, width, pie...  69.6 us
    pallas_call x1, Pallas kernels, per_device(): pl.pallas_call(put_out, out_shape=tuple((pltpu.HBM(x.shape, x.dtype) for...  4.2 us

profile of v2, /device:TPU:0, one launch (start us, length us, event | category | flops | bytes accessed | tf_op | source)
XLA Modules:
  0.0 74.4 jit_solution(10207252818062011786)
XLA Ops:
  0.6 69.6 %sum_update_gather.1 = (bf16[1024,3072]{1,0:T(8,128)(2,1)S(1)}, f32[128,3072]{1,0:T(8,128)S(1)}, f32[128,3072]{1,0:T(8,128)S(1)}, f32[128,3072]{1,0:T(8,128)S(1)}) custom-call(bf16[1024,3072]{1,0:T(8,128)(2,1)} %bitcast.7, f32[128,3072]{1,0:T(8,128)} %bitcast.8, f32[128,3072]{1,0:T(8,128)} %bitcast.9, f32[128,3072]{1,0:T(8,128)} %bitcast.10), custom_call_target="tpu_custom_call" | custom-call | tf_op jit(solution)/shard_map/sum_update_gather/pallas_call | solution.py:282
  70.2 4.2 %put_out.1 = (bf16[1024,3072]{1,0:T(8,128)(2,1)}, f32[128,3072]{1,0:T(8,128)}, f32[128,3072]{1,0:T(8,128)}, f32[128,3072]{1,0:T(8,128)}) custom-call(bf16[1024,3072]{1,0:T(8,128)(2,1)S(1)} %get-tuple-element.12.refs_0_, f32[128,3072]{1,0:T(8,128)S(1)} %get-tuple-element.13.refs_1_, f32[128,3072]{1,0:T(8,128)S(1)} %get-tuple-element.14.refs_2_, ...), custom_call_target="tpu_custom_call" | custom-call | tf_op jit(solution)/shard_map/put_out/pallas_call | solution.py:298
